TPU v7x, 32 devices: a whole 2x2x4 slice. The times are simulated.
32 devices in a mesh: gy: 8 (over z, y), gz: 4 (over x, core).
Axes of the slice: x: 2, y: 2, z: 4, core: 2. Of those that a mesh axis runs over, the one named last changes fastest.
Arguments:
- wavefunction: float32 [2, 8, 1024, 1024], P(None, None, 'gy', 'gz'), may hold values from -6 to 6
- absorber: float32 [8, 1024, 1024], P(None, 'gy', 'gz'), may hold values from 0.05 to 1.5
- row_inverse: float32 [2, 1024, 128], P(None, 'gy'), may hold values from -1 to 1
- column_inverse: float32 [2, 1024, 256], replicated, may hold values from -1 to 1
- link_terms: float32 [2, 2, 2], replicated, may hold values from 0.65 to 0.7
- shell_blocks: int32 [4, 8, 56], P('gz'), may hold values from 0 to 63, as said below
- owner_map: int32 [4, 8, 56, 1], P('gz'), may hold values from 0 to 7; in each aligned block of 56 rows (0 to 55, 56 to 111, ..., all dimensions but the last counted through in order) at most 14 rows name the same one
- volkov_phase: float32 [128, 128], replicated, may hold values from -3.140625 to 3.140625
Outputs:
- damped: float32 [2, 8, 1024, 1024], P(None, None, 'gy', 'gz')
- spectrum: float32 [2, 64, 512, 128], P(None, 'gy', 'gz')
Inputs may be any that keep to these rules, and one draw needn't show every extreme that they name: `shell_blocks`: the ids listed for one device are distinct. `owner_map`: at most 14 of one device's listed blocks name the same owner.
All inputs are finite; a program needn't handle non-finite values.
Results may differ from a plain program's by a relative error of at most 0.0003.
Values sent between devices are 32-bit elements; how exact they have to be, the bound alone decides.
No kernel may reach another device: no remote copies, remote signals or barrier semaphores. Data moves between devices by JAX's collectives and lax.ppermute only.
A program may use at most 64 MiB of HBM per device.

v0:
```python
import math

import jax
import jax.numpy as jnp
from jax import lax
from jax.sharding import PartitionSpec as P

BY = 2
KY = 128
KZ = 128


precise = lax.Precision.HIGHEST


def prefix(part, axis, combine, identity, reverse):
    count = lax.axis_size(axis)
    place = lax.axis_index(axis)
    ahead = count - 1 - place if reverse else place
    gathered = jax.tree.map(lambda a: lax.all_gather(a, axis), part)
    state = jax.tree.map(lambda a, e: jnp.zeros_like(a) + jnp.asarray(e, a.dtype), part, identity)

    def one(lap, state):
        source = count - 1 - lap if reverse else lap
        return combine(
            state, jax.tree.map(lambda a: lax.dynamic_index_in_dim(a, source, 0, False), gathered)
        )

    return lax.fori_loop(0, ahead, one, state)


def complex_mul(former, latter):
    return (
        former[0] * latter[0] - former[1] * latter[1],
        former[0] * latter[1] + former[1] * latter[0],
    )


def complex_div(former, latter):
    modulus = latter[0] * latter[0] + latter[1] * latter[1]
    return (
        (former[0] * latter[0] + former[1] * latter[1]) / modulus,
        (former[1] * latter[0] - former[0] * latter[1]) / modulus,
    )


def complex_add(former, latter):
    return (former[0] + latter[0], former[1] + latter[1])


def complex_sub(former, latter):
    return (former[0] - latter[0], former[1] - latter[1])


def complex_einsum(pattern, former, latter):
    real_part = jnp.einsum(pattern, former[0], latter[0], precision=precise) - jnp.einsum(
        pattern, former[1], latter[1], precision=precise
    )
    imag_part = jnp.einsum(pattern, former[0], latter[1], precision=precise) + jnp.einsum(
        pattern, former[1], latter[0], precision=precise
    )
    return (real_part, imag_part)


def phase_table(positions, count):
    wavenum = jnp.arange(count, dtype=jnp.int32)
    turns = positions[..., None] * wavenum % count
    parity = (positions[..., None] % 2).astype(jnp.float32)
    phases = 2.0 * math.pi / count * turns.astype(jnp.float32) - math.pi * parity
    return (jnp.cos(phases), -jnp.sin(phases))


def edge_terms(inverse, prev_link, next_link):
    length = inverse[0].shape[-1]
    left_spike = complex_mul(prev_link, (inverse[0][..., 0], inverse[1][..., 0]))
    right_spike = complex_mul(next_link, (inverse[0][..., length - 1], inverse[1][..., length - 1]))
    edges = (
        (left_spike[0][..., 0], left_spike[1][..., 0]),
        (left_spike[0][..., length - 1], left_spike[1][..., length - 1]),
        (right_spike[0][..., 0], right_spike[1][..., 0]),
        (right_spike[0][..., length - 1], right_spike[1][..., length - 1]),
    )
    return (left_spike, right_spike, edges)


def chain_local(edges, head_part, tail_part):
    unity = (jnp.ones((), jnp.float32), jnp.zeros((), jnp.float32))

    def forward(carry, inputs):
        coupling, carried = carry
        spikes, head_now, tail_now = inputs
        pivot_value = complex_sub(unity, complex_mul(spikes[0], coupling))
        gain_term = complex_div(spikes[1], pivot_value)
        coupling_next = complex_add(
            spikes[3], complex_mul(gain_term, complex_mul(spikes[2], coupling))
        )
        carried_next = complex_add(
            complex_mul(gain_term, carried),
            complex_add(tail_now, complex_mul(complex_mul(gain_term, coupling), head_now)),
        )
        return ((coupling_next, carried_next), (coupling, carried, pivot_value))

    zero_lines = (jnp.zeros_like(head_part[0][0]), jnp.zeros_like(head_part[0][0]))
    initial = ((jnp.zeros((), jnp.float32), jnp.zeros((), jnp.float32)), zero_lines)
    final_state, (coupling_prev, carried_prev, pivots) = lax.scan(
        forward, initial, (edges, head_part, tail_part)
    )

    def backward(head_next, inputs):
        spikes, head_now, carried_now, coupling_now, pivot_value = inputs
        offset = complex_div(
            complex_add(head_now, complex_mul(spikes[0], carried_now)), pivot_value
        )
        factor = complex_div(spikes[2], pivot_value)
        head_value = complex_add(offset, complex_mul(factor, head_next))
        left_value = complex_add(carried_now, complex_mul(coupling_now, head_value))
        return (head_value, (left_value, head_next))

    final_head, (left_values, right_values) = lax.scan(
        backward, zero_lines, (edges, head_part, carried_prev, coupling_prev, pivots), reverse=True
    )
    return (left_values, right_values)


def mobius_combine(earlier, latter):
    real_part = jnp.einsum("ij,jk->ik", latter[0], earlier[0], precision=precise) - jnp.einsum(
        "ij,jk->ik", latter[1], earlier[1], precision=precise
    )
    imag_part = jnp.einsum("ij,jk->ik", latter[0], earlier[1], precision=precise) + jnp.einsum(
        "ij,jk->ik", latter[1], earlier[0], precision=precise
    )
    return jnp.stack([real_part, imag_part])


def mobius_unit():
    return jnp.stack([jnp.eye(2, dtype=jnp.float32), jnp.zeros((2, 2), jnp.float32)])


def affine_combine(earlier, latter):
    joined = jnp.stack(
        [
            latter[0][0] * earlier[0][0] - latter[0][1] * earlier[0][1],
            latter[0][0] * earlier[0][1] + latter[0][1] * earlier[0][0],
        ]
    )
    moved_real = latter[0][0] * earlier[1][0] - latter[0][1] * earlier[1][1] + latter[1][0]
    moved_imag = latter[0][0] * earlier[1][1] + latter[0][1] * earlier[1][0] + latter[1][1]
    return (joined, jnp.stack([moved_real, moved_imag]))


def affine_unit(operand):
    return (
        jnp.stack([jnp.ones((), jnp.float32), jnp.zeros((), jnp.float32)]),
        jnp.zeros_like(operand[1]),
    )


def scan_chain(edges, head_part, tail_part, mobius_scan, affine_forward, affine_backward):
    lead_left, tail_left, lead_right, tail_right = edges
    unity = (jnp.ones((), jnp.float32), jnp.zeros((), jnp.float32))
    upper = complex_sub(complex_mul(tail_left, lead_right), complex_mul(tail_right, lead_left))
    matrix = jnp.stack(
        [
            jnp.stack([jnp.stack([upper[0], tail_right[0]]), jnp.stack([-lead_left[0], unity[0]])]),
            jnp.stack([jnp.stack([upper[1], tail_right[1]]), jnp.stack([-lead_left[1], unity[1]])]),
        ]
    )
    product = mobius_scan(matrix)
    coupling = complex_div(
        (product[0, 0, 1], product[1, 0, 1]), (product[0, 1, 1], product[1, 1, 1])
    )
    pivot_value = complex_sub(unity, complex_mul(lead_left, coupling))
    gain_term = complex_div(tail_left, pivot_value)
    source = complex_add(tail_part, complex_mul(complex_mul(gain_term, coupling), head_part))
    carried = affine_forward(
        (jnp.stack([gain_term[0], gain_term[1]]), jnp.stack([source[0], source[1]]))
    )
    carried_prev = (carried[0], carried[1])
    offset = complex_div(complex_add(head_part, complex_mul(lead_left, carried_prev)), pivot_value)
    factor = complex_div(lead_right, pivot_value)
    following = affine_backward(
        (jnp.stack([factor[0], factor[1]]), jnp.stack([offset[0], offset[1]]))
    )
    head_next = (following[0], following[1])
    head_value = complex_add(offset, complex_mul(factor, head_next))
    left_value = complex_add(carried_prev, complex_mul(coupling, head_value))
    return (left_value, head_next)


def body(
    wavefunction,
    absorber,
    row_inverse,
    column_inverse,
    link_terms,
    shell_blocks,
    owner_map,
    volkov_phase,
):
    rows_x, width_y, width_z = (wavefunction.shape[1], wavefunction.shape[2], wavefunction.shape[3])
    row_rank = lax.axis_index("gy")
    column_rank = lax.axis_index("gz")
    row_devices = lax.axis_size("gy")
    column_devices = lax.axis_size("gz")
    row_block = (row_inverse[0], row_inverse[1])
    row_left, row_right, row_edges = edge_terms(
        row_block,
        (link_terms[0, 0, 0], link_terms[0, 0, 1]),
        (link_terms[0, 1, 0], link_terms[0, 1, 1]),
    )
    solved = complex_einsum("ab,xbz->xaz", row_block, (wavefunction[0], wavefunction[1]))
    head_part = (solved[0][:, 0], solved[1][:, 0])
    tail_part = (solved[0][:, width_y - 1], solved[1][:, width_y - 1])
    left_value, right_value = scan_chain(
        row_edges,
        head_part,
        tail_part,
        lambda operand: prefix(operand, "gy", mobius_combine, mobius_unit(), False),
        lambda operand: prefix(operand, "gy", affine_combine, affine_unit(operand), False)[1],
        lambda operand: prefix(operand, "gy", affine_combine, affine_unit(operand), True)[1],
    )
    field_y = complex_add(
        solved,
        complex_add(
            complex_mul(
                (row_left[0][None, :, None], row_left[1][None, :, None]),
                (left_value[0][:, None, :], left_value[1][:, None, :]),
            ),
            complex_mul(
                (row_right[0][None, :, None], row_right[1][None, :, None]),
                (right_value[0][:, None, :], right_value[1][:, None, :]),
            ),
        ),
    )
    column_prev = (link_terms[1, 0, 0], link_terms[1, 0, 1])
    column_next = (link_terms[1, 1, 0], link_terms[1, 1, 1])
    column_all = (
        column_inverse[0].reshape(column_devices, width_z, width_z),
        column_inverse[1].reshape(column_devices, width_z, width_z),
    )
    column_left, column_right, column_edges = edge_terms(column_all, column_prev, column_next)
    pieces = (
        lax.all_to_all(field_y[0], "gz", split_axis=0, concat_axis=2, tiled=True),
        lax.all_to_all(field_y[1], "gz", split_axis=0, concat_axis=2, tiled=True),
    )
    planes, columns, length_z = pieces[0].shape
    grouped = (
        pieces[0].reshape(planes, columns, column_devices, width_z),
        pieces[1].reshape(planes, columns, column_devices, width_z),
    )
    solved_lines = complex_einsum("jab,xyjb->xyja", column_all, grouped)
    head_lines = (
        jnp.moveaxis(solved_lines[0][..., 0], 2, 0),
        jnp.moveaxis(solved_lines[1][..., 0], 2, 0),
    )
    tail_lines = (
        jnp.moveaxis(solved_lines[0][..., width_z - 1], 2, 0),
        jnp.moveaxis(solved_lines[1][..., width_z - 1], 2, 0),
    )
    left_lines, right_lines = chain_local(column_edges, head_lines, tail_lines)
    lifted = complex_add(
        solved_lines,
        complex_add(
            complex_mul(
                (column_left[0][None, None], column_left[1][None, None]),
                (
                    jnp.moveaxis(left_lines[0], 0, 2)[..., None],
                    jnp.moveaxis(left_lines[1], 0, 2)[..., None],
                ),
            ),
            complex_mul(
                (column_right[0][None, None], column_right[1][None, None]),
                (
                    jnp.moveaxis(right_lines[0], 0, 2)[..., None],
                    jnp.moveaxis(right_lines[1], 0, 2)[..., None],
                ),
            ),
        ),
    )
    field_z = (
        lax.all_to_all(
            lifted[0].reshape(planes, columns, length_z),
            "gz",
            split_axis=2,
            concat_axis=0,
            tiled=True,
        ),
        lax.all_to_all(
            lifted[1].reshape(planes, columns, length_z),
            "gz",
            split_axis=2,
            concat_axis=0,
            tiled=True,
        ),
    )
    kept = jnp.exp(-absorber)
    damped = (field_z[0] * kept, field_z[1] * kept)
    lost = (field_z[0] - damped[0], field_z[1] - damped[1])
    blocks_dev = width_y // BY
    shell_dev = shell_blocks.shape[2]
    capacity = 2 * ((shell_dev + row_devices - 1) // row_devices)
    slots = row_devices * capacity
    listed = shell_blocks[0]
    targets = owner_map[0, :, :, 0]
    own_ids = lax.dynamic_index_in_dim(listed, row_rank, 0, keepdims=False)
    own_targets = lax.dynamic_index_in_dim(targets, row_rank, 0, keepdims=False)
    earlier_mask = (
        jnp.arange(shell_dev, dtype=jnp.int32)[:, None]
        > jnp.arange(shell_dev, dtype=jnp.int32)[None, :]
    )
    rank_own = jnp.sum((own_targets[:, None] == own_targets[None, :]) & earlier_mask, axis=1)
    slot_own = own_targets * capacity + rank_own
    placing = (jnp.arange(slots, dtype=jnp.int32)[:, None] == slot_own[None, :]).astype(jnp.float32)
    picking = (own_ids[:, None] == jnp.arange(blocks_dev, dtype=jnp.int32)[None, :]).astype(
        jnp.float32
    )
    lost_blocks = (
        lost[0].reshape(rows_x, blocks_dev, BY, width_z),
        lost[1].reshape(rows_x, blocks_dev, BY, width_z),
    )
    z_table = phase_table(column_rank * width_z + jnp.arange(width_z, dtype=jnp.int32), KZ)
    mine = targets == row_rank
    rank_source = jnp.sum(mine[:, None, :] & earlier_mask[None], axis=2)
    hitting = mine[:, None, :] & (
        rank_source[:, None, :] == jnp.arange(capacity, dtype=jnp.int32)[None, :, None]
    )
    block_of = jnp.sum(jnp.where(hitting, listed[:, None, :], 0), axis=2)
    rows_y = (
        jnp.arange(row_devices, dtype=jnp.int32)[:, None, None] * width_y
        + block_of[:, :, None] * BY
        + jnp.arange(BY, dtype=jnp.int32)[None, None, :]
    ).reshape(slots, BY)
    y_table = phase_table(rows_y, KY)
    routing = jnp.dot(placing, picking, precision=precise)
    outgoing = tuple(
        (jnp.einsum("rk,xkbz->rxbz", routing, member, precision=precise) for member in lost_blocks)
    )
    moved = complex_einsum(
        "rxbz,zq->rxbq",
        (
            lax.all_to_all(outgoing[0], "gy", split_axis=0, concat_axis=0, tiled=True),
            lax.all_to_all(outgoing[1], "gy", split_axis=0, concat_axis=0, tiled=True),
        ),
        z_table,
    )
    spectra = complex_einsum("rbk,rxbq->xkq", y_table, moved)
    phased = complex_mul((jnp.cos(volkov_phase), jnp.sin(volkov_phase)), spectra)
    weight_norm = 1.0 / math.sqrt(width_y * width_z)
    spectrum = jnp.stack([phased[0], phased[1]]) * weight_norm
    return (jnp.stack([damped[0], damped[1]]), spectrum)


def solution(mesh):
    placed = (
        P(None, None, "gy", "gz"),
        P(None, "gy", "gz"),
        P(None, "gy", None),
        P(),
        P(),
        P("gz", None, None),
        P("gz", None, None, None),
        P(),
    )
    return jax.shard_map(
        body,
        mesh=mesh,
        in_specs=placed,
        out_specs=(P(None, None, "gy", "gz"), P(None, "gy", "gz", None)),
        check_vma=False,
    )
```

profile of v0, /device:TPU:0, one launch (start us, length us, event | category | flops | bytes accessed | tf_op | source)
XLA Modules:
  0.0 528.7 jit_solution(2287570947758042175)
XLA Ops:
  0.7 1.6 fusion.168
  3.1 2.8 fusion.155
  19.9 27.9 %all-gather = f32[16,2,2]{2,1,0:T(2,128)S(1)} all-gather(f32[2,2,2]{2,1,0:T(2,128)S(1)} %pad_maximum_fusion.6), channel_id=2, replica_groups=mesh['gy'=8,'gz'=4] {'gy'}, dimensions={0}, use_global_device_ids=true | all-gather | bytes 288 | tf_op jit(solution)/shard_map/all_gather | solution.py:20
  63.6 3.3 fusion.46
  66.9 2.0 fusion.50
  70.7 23.9 %all-reduce.3 = (f32[16]{0:T(128)S(1)}, f32[16]{0:T(128)S(1)}) all-reduce(f32[16]{0:T(128)S(1)} %maximum_dynamic-update-slice_fusion.1, f32[16]{0:T(128)S(1)} %maximum_dynamic-update-slice_fusion), channel_id=5, replica_groups=mesh['gy'=8,'gz'=4] {'gy'}, use_global_device_ids=true, to_apply=%add.2 | all-reduce | flops 32 | bytes 256
  94.7 2.4 fusion.34
  97.1 2.0 fusion.35
  100.2 30.5 %all-gather.2 = f32[16,8,256]{2,1,0:T(8,128)S(1)} all-gather(f32[2,8,256]{2,1,0:T(8,128)S(1)} %copy.194), channel_id=4, replica_groups=mesh['gy'=8,'gz'=4] {'gy'}, dimensions={0}, use_global_device_ids=true | all-gather | bytes 147456 | tf_op jit(solution)/shard_map/all_gather | solution.py:20
  130.7 2.1 fusion.112
  132.8 2.1 add_divide_fusion
  135.1 38.9 %all-gather.4 = f32[16,8,256]{2,1,0:T(8,128)S(1)} all-gather(f32[2,8,256]{2,1,0:T(8,128)S(1)} %copy.198), channel_id=6, replica_groups=mesh['gy'=8,'gz'=4] {'gy'}, dimensions={0}, use_global_device_ids=true | all-gather | bytes 147456 | tf_op jit(solution)/shard_map/all_gather | solution.py:20
  174.0 13.0 %while.92 = (s32[]{:T(128)}, f32[2,8,256]{2,1,0:T(8,128)S(1)}, s32[]{:T(128)}, f32[8,2]{1,0:T(8,128)S(1)}, f32[8,2,8,256]{3,2,1,0:T(8,128)S(1)}, /*index=5*/s32[]{:T(128)}, s32[]{:T(128)}, s32[]{:T(128)}, s32[]{:T(128)}, s32[]{}) while((s32[]{:T(128)}, f32[2,8,256]{2,1,0:T(8,128)S(1)}, s32[]{:T(128)}, f32[8,2]{1,0:T(8,128)S(1)}, ...), condition=%wide.region_5.6_spmd, body=%wide.region_4.5_spmd.sunk | while | flops 20487 | bytes 82139 | solution.py:29
  187.2 1.6 add_add_fusion.3
  188.8 17.0 %all_to_all.76 = f32[8,128,256]{2,1,0:T(8,128)S(1)} all-to-all(f32[8,128,256]{2,1,0:T(8,128)S(1)} %get-tuple-element.1294), channel_id=1, replica_groups=mesh['gy'=8,'gz'=4] {'gz'}, dimensions={0} | all-to-all | bytes 2097152 | tf_op jit(solution)/shard_map/all_to_all | solution.py:244
  205.8 4.5 all-to-all-start
  210.3 1.7 fusion.159
  212.1 3.4 add_reduce_fusion
  216.0 2.1 fusion.175
  218.1 6.7 %all-to-all-done = f32[8,128,256]{2,1,0:T(8,128)} async-done(((f32[8,128,256]{2,1,0:T(8,128)}), f32[8,128,256]{2,1,0:T(8,128)}, u32[]{:S(2)}, u32[]{:S(2)}) %all-to-all-start) | async-done | bytes 1048608 | tf_op jit(solution)/shard_map/all_to_all | solution.py:243
  224.8 2.5 fusion.174
  227.3 2.4 fusion.32
  233.1 59.9 %while.93 = (s32[]{:T(128)}, f32[]{:T(128)}, f32[]{:T(128)}, f32[2,128]{1,0:T(2,128)S(1)}, f32[2,128]{1,0:T(2,128)S(1)}, /*index=5*/f32[4]{0:T(128)S(1)}, f32[4]...) while((s32[]{:T(128)}, f32[]{:T(128)}, f32[]{:T(128)}, ...), condition=%wide.region_7.8_spmd.clone, body=%wide.region_6.7_spmd.clone.sunk | while | flops 5162 | bytes 17296 | solution.py:105
  293.1 70.1 %while.94 = (s32[]{:T(128)}, f32[2,128]{1,0:T(2,128)S(1)}, f32[2,128]{1,0:T(2,128)S(1)}, f32[4,2,128]{2,1,0:T(2,128)S(1)}, f32[4,2,128]{2,1,0:T(2,128)S(1)}, /*i...) while((s32[]{:T(128)}, f32[2,128]{1,0:T(2,128)S(1)}, ...), condition=%wide.region_9.10_spmd.clone, body=%wide.region_8.9_spmd.clone.sunk | while | flops 8719 | bytes 20991 | solution.py:119
  305.5 1.2 fusion.211
  306.7 2.5 constant_dynamic-update-slice_fusion.10
  309.3 1.3 constant_dynamic-update-slice_fusion.11
  323.0 1.2 fusion.211
  324.2 2.5 constant_dynamic-update-slice_fusion.10
  326.8 1.3 constant_dynamic-update-slice_fusion.11
  341.8 2.5 constant_dynamic-update-slice_fusion.10
  344.3 1.3 constant_dynamic-update-slice_fusion.11
  359.3 2.5 constant_dynamic-update-slice_fusion.10
  361.8 1.3 constant_dynamic-update-slice_fusion.11
  363.2 1.6 add_add_fusion.1
  364.8 1.5 copy.212
  366.3 1.8 copy.213
  368.1 3.5 all-to-all-start.2
  372.0 1.8 copy.217
  373.8 12.3 %all-to-all-done.2 = f32[2,128,1024]{1,0,2:T(2,128)S(1)} async-done(((f32[2,128,1024]{1,0,2:T(2,128)}), f32[2,128,1024]{1,0,2:T(2,128)S(1)}, u32[]{:S(2)}, u32[]{:S(2)}) %all-to-all-start.2) | async-done | bytes 1048608 | tf_op jit(solution)/shard_map/all_to_all | solution.py:281
  386.0 4.0 all-to-all-start.3
  391.0 13.5 %all-to-all-done.3 = f32[2,128,1024]{1,0,2:T(2,128)S(1)} async-done(((f32[2,128,1024]{1,0,2:T(2,128)}), f32[2,128,1024]{1,0,2:T(2,128)S(1)}, u32[]{:S(2)}, u32[]{:S(2)}) %all-to-all-start.3) | async-done | bytes 1048608 | tf_op jit(solution)/shard_map/all_to_all | solution.py:288
  404.5 1.3 copy.219
  405.8 3.6 bitcast_subtract_fusion.1
  409.4 1.8 reshape.562
  411.3 1.6 fusion.52
  412.9 2.6 copy.225
  415.6 3.6 all-to-all-start.5
  419.2 1.6 reshape.561
  420.7 2.9 fusion.54
  423.6 2.6 copy.222
  426.3 35.4 %all-to-all-done.5 = f32[112,8,2,256]{3,2,1,0:T(2,128)S(1)} async-done(((f32[112,8,2,256]{3,2,1,0:T(2,128)}), f32[112,8,2,256]{3,2,1,0:T(2,128)S(1)}, u32[]{:S(2)}, u32[]{:S(2)}) %all-to-all-start.5) | async-done | bytes 1835040 | tf_op jit(solution)/shard_map/all_to_all | solution.py:342
  461.7 4.5 all-to-all-start.4
  467.5 2.7 pad_maximum_fusion.3
  470.2 2.1 fusion.24
  472.4 35.8 %all-to-all-done.4 = f32[112,8,2,256]{3,2,1,0:T(2,128)} async-done(((f32[112,8,2,256]{3,2,1,0:T(2,128)}), f32[112,8,2,256]{3,2,1,0:T(2,128)}, u32[]{:S(2)}, u32[]{:S(2)}) %all-to-all-start.4) | async-done | bytes 1835040 | tf_op jit(solution)/shard_map/all_to_all | solution.py:341
  508.2 3.6 fusion.39
  511.8 2.3 convolution_bitcast_fusion.2
  514.2 2.1 fusion.26
  516.3 3.6 fusion.36
  519.9 2.5 convolution_bitcast_fusion
  522.5 2.3 fusion.43
  524.8 2.3 subtract_bitcast_fusion
  527.2 1.3 copy.235
  (236 shorter events, 70.0 us)
Async XLA Ops:
  0.6 66.2 %copy-start.7 = (f32[2,128,128]{2,1,0:T(8,128)S(1)}, f32[2,128,128]{2,1,0:T(8,128)}, u32[]{:S(2)}) copy-start(f32[2,128,128]{2,1,0:T(8,128)} %param.20) | copy-start | bytes 393220
  0.6 66.2 %copy-start.2 = (f32[2,8,128,256]{3,2,1,0:T(8,128)S(1)}, f32[2,8,128,256]{3,2,1,0:T(8,128)}, u32[]{:S(2)}) copy-start(f32[2,8,128,256]{3,2,1,0:T(8,128)} %param.18) | copy-start | bytes 6291460
  63.6 5.5 %copy-start.11 = (u32[32]{0:T(128)S(1)}, u32[32]{0:T(128)}, u32[]{:S(2)}) copy-start(u32[32]{0:T(128)} %constant.215) | copy-start | bytes 388
  94.7 2.4 copy-start.4
  99.1 88.1 %copy-start.3 = (f32[8,128,256]{2,1,0:T(8,128)S(1)}, f32[8,128,256]{2,1,0:T(8,128)}, u32[]{:S(2)}) copy-start(f32[8,128,256]{2,1,0:T(8,128)} %fusion.35) | copy-start | bytes 3145732
  205.8 19.0 %all-to-all-start = ((f32[8,128,256]{2,1,0:T(8,128)}), f32[8,128,256]{2,1,0:T(8,128)}, u32[]{:S(2)}, u32[]{:S(2)}) async-start(f32[8,128,256]{2,1,0:T(8,128)} %get-tuple-element.1293), calls=%async_computation | async-start | bytes 2097152 | tf_op jit(solution)/shard_map/all_to_all | solution.py:243
  224.8 2.5 copy-start.6
  230.9 1.0 copy-start
  232.7 130.5 %copy-start.1 = (f32[2,128,4,256]{3,1,0,2:T(8,128)S(1)}, f32[2,128,4,256]{3,1,0,2:T(8,128)}, u32[]{:S(2)}) copy-start(f32[2,128,4,256]{3,1,0,2:T(8,128)} %copy-done) | copy-start | bytes 3145732
  368.1 17.9 %all-to-all-start.2 = ((f32[2,128,1024]{1,0,2:T(2,128)}), f32[2,128,1024]{1,0,2:T(2,128)S(1)}, u32[]{:S(2)}, u32[]{:S(2)}) async-start(f32[2,128,1024]{1,0,2:T(2,128)} %copy.213), calls=%async_computation.2 | async-start | bytes 2097152 | tf_op jit(solution)/shard_map/all_to_all | solution.py:281
  372.0 18.1 %copy-start.10 = (s32[1,8,56]{2,1,0:T(8,128)S(1)}, s32[1,8,56]{2,1,0:T(8,128)}, u32[]{:S(2)}) copy-start(s32[1,8,56]{2,1,0:T(8,128)} %param.23) | copy-start | bytes 5380
  372.0 18.1 %copy-start.9 = (s32[1,8,56,1]{2,3,1,0:T(1,128)S(1)}, s32[1,8,56,1]{2,3,1,0:T(1,128)}, u32[]{:S(2)}) copy-start(s32[1,8,56,1]{2,3,1,0:T(1,128)} %param.24) | copy-start | bytes 5380
  386.0 18.4 %all-to-all-start.3 = ((f32[2,128,1024]{1,0,2:T(2,128)}), f32[2,128,1024]{1,0,2:T(2,128)S(1)}, u32[]{:S(2)}, u32[]{:S(2)}) async-start(f32[2,128,1024]{1,0,2:T(2,128)} %copy.217), calls=%async_computation.3 | async-start | bytes 2097152 | tf_op jit(solution)/shard_map/all_to_all | solution.py:288
  415.6 46.1 %all-to-all-start.5 = ((f32[112,8,2,256]{3,2,1,0:T(2,128)}), f32[112,8,2,256]{3,2,1,0:T(2,128)S(1)}, u32[]{:S(2)}, u32[]{:S(2)}) async-start(f32[112,8,2,256]{3,2,1,0:T(2,128)} %copy.225), calls=%async_computation.5 | async-start | bytes 3670016 | tf_op jit(solution)/shard_map/all_to_all | solution.py:342
  426.3 40.7 %copy-start.8 = (f32[128,128]{1,0:T(8,128)S(1)}, f32[128,128]{1,0:T(8,128)}, u32[]{:S(2)}) copy-start(f32[128,128]{1,0:T(8,128)} %param.25) | copy-start | bytes 196612
  426.3 41.2 %copy-start.5 = (f32[8,128,256]{2,1,0:T(8,128)S(1)}, f32[8,128,256]{2,1,0:T(8,128)}, u32[]{:S(2)}) copy-start(f32[8,128,256]{2,1,0:T(8,128)} %get-tuple-element.1260) | copy-start | bytes 3145732
  461.7 46.5 %all-to-all-start.4 = ((f32[112,8,2,256]{3,2,1,0:T(2,128)}), f32[112,8,2,256]{3,2,1,0:T(2,128)}, u32[]{:S(2)}, u32[]{:S(2)}) async-start(f32[112,8,2,256]{3,2,1,0:T(2,128)} %copy.222), calls=%async_computation.4 | async-start | bytes 3670016 | tf_op jit(solution)/shard_map/all_to_all | solution.py:341
where the time goes:
time: 537 us; the launch traced here: 529 us
  blocking collectives  138 us (26%)
  waiting for transfers between devices  104 us (19%)
  local copies, waits for them, and re-layouts  73.3 us (14%)
  loops' own time  68 us (13%)
  other arithmetic  53 us (10%)
  matrix products  43.6 us (8%)
  between operations  28.7 us (5%)
  starting transfers between devices  20.2 us (4%)
    all_gather x3, blocking collectives, prefix(): gathered = jax.tree.map(lambda a: lax.all_gather(a, axis), part)  97.3 us
    dynamic_slice x68, local copies, waits for them, and re-layouts, chain_local(): lax.scan(forward, initial, (edges, head_part, tail_part))  39.9 us
    another operation x1, loops' own time, chain_local(): lax.scan(forward, initial, (edges, head_part, tail_part))  37.7 us
    all_to_all x1, waiting for transfers between devices, body(): lax.all_to_all(outgoing[0], 'gy', split_axis=0, concat_axis=0, tiled=True)  35.8 us
    all_to_all x1, waiting for transfers between devices, body(): lax.all_to_all(outgoing[1], 'gy', split_axis=0, concat_axis=0, tiled=True)  35.4 us
    another operation x1, loops' own time, chain_local(): lax.scan(backward, zero_lines, (edges, head_part, carried_prev, coupling_...  30 us
    unnamed x1, blocking collectives  23.9 us
    all_to_all x1, blocking collectives, body(): lax.all_to_all(field_y[1], 'gz', split_axis=0, concat_axis=2, tiled=True)  17 us
  transfers between devices with their start and end apart: 5, of which 5 were waited for; matrix products, arithmetic and copies ran while one was open for 5% of the time, Pallas kernels for 0%

commit v1 on v0

v1 whole, which is shorter than its diff:
```python
import math

import jax
import jax.numpy as jnp
import numpy as np
from jax import lax
from jax.experimental import pallas as pl
from jax.experimental.pallas import tpu as pltpu
from jax.sharding import PartitionSpec as P

BY = 2
KY = 128
KZ = 128
EDGE = 8
CHUNKS = 1

f32 = jnp.float32
bf16 = jnp.bfloat16
NN = (((1,), (0,)), ((), ()))
NT = (((1,), (1,)), ((), ()))
TN = (((0,), (0,)), ((), ()))


def mm(a, b, dims=NN):
    return lax.dot_general(a, b, dims, preferred_element_type=f32)


def split(a):
    hi = a.astype(bf16)
    return hi, (a - hi.astype(f32)).astype(bf16)


def mm3(a, b, dims=NN):
    return mm(a[0], b[0], dims) + mm(a[0], b[1], dims) + mm(a[1], b[0], dims)


def cmul(a, b):
    return (a[0] * b[0] - a[1] * b[1], a[0] * b[1] + a[1] * b[0])


def cdiv(a, b):
    modulus = b[0] * b[0] + b[1] * b[1]
    return ((a[0] * b[0] + a[1] * b[1]) / modulus, (a[1] * b[0] - a[0] * b[1]) / modulus)


def cadd(a, b):
    return (a[0] + b[0], a[1] + b[1])


def put(hi_ref, lo_ref, rows, cols, value):
    hi, lo = split(value)
    hi_ref[rows, cols] = hi
    lo_ref[rows, cols] = lo


def spikes_of(transposed, link, sweep):
    last = transposed[0].shape[0] - 1
    left = cmul(
        (link[sweep, 0, 0], link[sweep, 0, 1]), (transposed[0][0:1], transposed[1][0:1])
    )
    right = cmul(
        (link[sweep, 1, 0], link[sweep, 1, 1]),
        (transposed[0][last : last + 1], transposed[1][last : last + 1]),
    )
    return left, right


def edge_rows(left, right, lanes):
    last = left[0].shape[1] - 1
    rows = []
    for spike in (left, right):
        for at in (0, last):
            for part in spike:
                rows.append(jnp.broadcast_to(part[:, at : at + 1], (1, lanes)))
    return rows


def solve_rows_kernel(link, w, y, thi, tlo, pay, spk, yh, yl, ps):
    x = pl.program_id(0)
    planes = pl.num_programs(0)
    n = y.shape[1]
    width = w.shape[3]

    @pl.when(x == 0)
    def _():
        yr = y[0]
        yi = y[1]
        put(yh, yl, slice(0, n), slice(0, n), yr)
        put(yh, yl, slice(0, n), slice(n, 2 * n), -yi)
        put(yh, yl, slice(n, 2 * n), slice(0, n), yi)
        put(yh, yl, slice(n, 2 * n), slice(n, 2 * n), yr)
        left, right = spikes_of((yr.T, yi.T), link, 0)
        for at, row in enumerate((left[0], left[1], right[0], right[1])):
            spk[at : at + 1, :] = row
        spk[4:8, :] = jnp.zeros((4, n), f32)
        count = ps.shape[0] - EDGE
        for at, row in enumerate(edge_rows(left, right, width)):
            ps[count + at : count + at + 1, :] = row

    wx = split(w[...].reshape(2 * n, width))
    t = mm3((yh[...], yl[...]), wx)
    hi, lo = split(t)
    thi[0, :, 0:width] = hi[0:n]
    thi[0, :, width : 2 * width] = hi[n : 2 * n]
    tlo[0, :, 0:width] = lo[0:n]
    tlo[0, :, width : 2 * width] = lo[n : 2 * n]
    nx = (ps.shape[0] - EDGE) // 4
    for at, row in enumerate((0, n, n - 1, 2 * n - 1)):
        ps[pl.ds(at * nx + x, 1), :] = t[row : row + 1]

    @pl.when(x == planes - 1)
    def _():
        value = ps[...]
        for g in range(pay.shape[0]):
            pay[g] = value


def solve_columns_kernel(link, thi, tlo, col, s, base, zh, zl, zsp, zed, zv, eh, el, sem):
    x = pl.program_id(0)
    wz = zv.shape[1]
    nx = base.shape[0] // 4

    @pl.when(x == 0)
    def _():
        rank = lax.axis_index("gz")
        copy = pltpu.make_async_copy(col.at[:, pl.ds(rank * wz, wz), :], zv, sem)
        copy.start()
        copy.wait()
        zr = zv[0]
        zi = zv[1]
        rt = zr.T
        it = zi.T
        put(zh, zl, slice(0, wz), slice(0, wz), rt)
        put(zh, zl, slice(0, wz), slice(wz, 2 * wz), it)
        put(zh, zl, slice(wz, 2 * wz), slice(0, wz), -it)
        put(zh, zl, slice(wz, 2 * wz), slice(wz, 2 * wz), rt)
        left, right = spikes_of((rt, it), link, 1)
        for at, spike in enumerate((left, right)):
            zsp[2 * at : 2 * at + 1, 0:wz] = spike[0]
            zsp[2 * at : 2 * at + 1, wz : 2 * wz] = spike[1]
            zsp[2 * at + 1 : 2 * at + 2, 0:wz] = -spike[1]
            zsp[2 * at + 1 : 2 * at + 2, wz : 2 * wz] = spike[0]
        zsp[4:8, :] = jnp.zeros((4, 2 * wz), f32)
        for at, row in enumerate(edge_rows(left, right, zed.shape[1])):
            zed[at : at + 1, :] = row
        zero = jnp.zeros((12, wz), f32)
        real = jnp.concatenate([zr[0:1], zi[0:1], zr[wz - 1 : wz], zi[wz - 1 : wz], zero], 0)
        imag = jnp.concatenate([-zi[0:1], zr[0:1], -zi[wz - 1 : wz], zr[wz - 1 : wz], zero], 0)
        put(eh, el, slice(0, 16), slice(0, wz), real)
        put(eh, el, slice(0, 16), slice(wz, 2 * wz), imag)

    t = (thi[0], tlo[0])
    s[0] = mm3(t, (zh[...], zl[...]))
    edges = mm3((eh[...], el[...]), t, NT)
    for at in range(4):
        base[pl.ds(at * nx + x, 1), :] = edges[at : at + 1]


def chain(gathered, nx, own, keep):
    groups = gathered.shape[0]
    lanes = gathered.shape[2]
    zero = jnp.zeros((nx, lanes), f32)

    def read(j):
        block = gathered[j]
        rows = [block[at * nx : (at + 1) * nx] for at in range(4)]
        edges = [
            jnp.broadcast_to(block[4 * nx + at : 4 * nx + at + 1], (nx, lanes))
            for at in range(EDGE)
        ]
        head, tail = (rows[0], rows[1]), (rows[2], rows[3])
        return head, tail, [(edges[2 * at], edges[2 * at + 1]) for at in range(4)]

    def forward(j, carry):
        coupling, carried = (carry[0], carry[1]), (carry[2], carry[3])
        head, tail, (lead_left, tail_left, lead_right, tail_right) = read(j)
        product = cmul(lead_left, coupling)
        pivot = (1.0 - product[0], -product[1])
        gain = cdiv(tail_left, pivot)
        for at, value in enumerate(coupling + carried + pivot):
            keep[j, at * nx : (at + 1) * nx, :] = value
        coupling_next = cadd(tail_right, cmul(gain, cmul(lead_right, coupling)))
        carried_next = cadd(
            cmul(gain, carried), cadd(tail, cmul(cmul(gain, coupling), head))
        )
        return coupling_next + carried_next

    def solved(j, head_next):
        head, _, (lead_left, _, lead_right, _) = read(j)
        kept = keep[j]
        values = [kept[at * nx : (at + 1) * nx] for at in range(6)]
        coupling, carried, pivot = (
            (values[0], values[1]),
            (values[2], values[3]),
            (values[4], values[5]),
        )
        offset = cdiv(cadd(head, cmul(lead_left, carried)), pivot)
        factor = cdiv(lead_right, pivot)
        value = cadd(offset, cmul(factor, head_next))
        return value, cadd(carried, cmul(coupling, value))

    lax.fori_loop(0, groups, forward, (zero, zero, zero, zero))
    following = lax.fori_loop(
        0,
        groups - 1 - own,
        lambda lap, head_next: solved(groups - 1 - lap, head_next)[0],
        (zero, zero),
    )
    return solved(own, following)[1], following


def row_chain_kernel(gathered, zh, zl, base, zed, spk, lam, pay, keep):
    nx = base.shape[0] // 4
    left, right = chain(gathered, nx, lax.axis_index("gy"), keep)
    stacked = jnp.concatenate(
        [jnp.concatenate([left[0], left[1]], 1), jnp.concatenate([right[0], right[1]], 1)], 0
    )
    moved = mm3(split(stacked), (zh[...], zl[...]))
    lam[...] = moved
    wz = moved.shape[1] // 2
    spikes = (
        (spk[0:1, :], spk[1:2, :]),
        (spk[2:3, :], spk[3:4, :]),
    )
    for at, z in enumerate((0, wz - 1)):
        value = (base[2 * at * nx : (2 * at + 1) * nx, :], base[(2 * at + 1) * nx : (2 * at + 2) * nx, :])
        for side in range(2):
            rows = slice(side * nx, (side + 1) * nx)
            factor = (moved[rows, z : z + 1], moved[rows, wz + z : wz + z + 1])
            value = cadd(value, cmul(factor, spikes[side]))
        pay[2 * at * nx : (2 * at + 1) * nx, :] = value[0]
        pay[(2 * at + 1) * nx : (2 * at + 2) * nx, :] = value[1]
    pay[4 * nx : 4 * nx + EDGE, :] = zed[...]


def route_kernel(listed, owners, place, *, tail):
    me = lax.axis_index("gy")
    groups, count = owners.shape
    rows = place.shape[1] // groups
    ny = place.shape[2] // 2
    ids = listed[pl.ds(me, 1), :]
    own = owners[pl.ds(me, 1), :]
    hot = (lax.broadcasted_iota(jnp.int32, (groups, count), 0) == own).astype(f32)
    upper = (
        lax.broadcasted_iota(jnp.int32, (count, count), 0)
        < lax.broadcasted_iota(jnp.int32, (count, count), 1)
    ).astype(bf16)
    earlier = mm(hot.astype(bf16), upper)
    rank = jnp.sum(hot * earlier, axis=0, keepdims=True).astype(jnp.int32)
    at = lax.broadcasted_iota(jnp.int32, (groups * rows, count), 0)
    n = lax.broadcasted_iota(jnp.int32, (ny, count), 0)
    for side in range(place.shape[0]):
        total = jnp.zeros((groups * rows, ny), f32)
        for b in range(BY):
            row = rank * BY + b
            if tail is not None and side:
                row = row + jnp.where(row >= tail, 4, 0)
            here = (at == own * rows + row).astype(f32).astype(bf16)
            there = (n == ids * BY + b).astype(f32).astype(bf16)
            total = total + mm(here, there, NT)
        place[side, :, 0:ny] = total.astype(bf16)
        place[side, :, ny : 2 * ny] = total.astype(bf16)


def table_kernel(listed, owners, table, phase, yt, vol, q, *, tail, norm):
    me = lax.axis_index("gy")
    groups, count = owners.shape
    rows = yt.shape[3] // groups
    ny = table.shape[2]
    mine = (owners[...] == me).astype(f32)
    upper = (
        lax.broadcasted_iota(jnp.int32, (count, count), 0)
        < lax.broadcasted_iota(jnp.int32, (count, count), 1)
    ).astype(f32).astype(bf16)
    rank = mm(mine.astype(bf16), upper).astype(jnp.int32)
    at = lax.broadcasted_iota(jnp.int32, (rows, count), 0)
    n = lax.broadcasted_iota(jnp.int32, (ny, count), 0)
    for side in range(yt.shape[0]):
        for g in range(groups):
            total = jnp.zeros((rows, ny), f32)
            for b in range(BY):
                row = rank[g : g + 1] * BY + b
                if tail is not None and side:
                    row = row + jnp.where(row >= tail, 4, 0)
                here = jnp.where(at == row, jnp.broadcast_to(mine[g : g + 1], at.shape), 0.0)
                there = (n == listed[g : g + 1, :] * BY + b).astype(f32).astype(bf16)
                total = total + mm(here.astype(bf16), there, NT)
            q[g * rows : (g + 1) * rows, :] = total.astype(bf16)
        for part in range(2):
            yt[side, part] = mm(table[part], q[...], NT).astype(bf16)
    vol[0] = jnp.cos(phase[...]) * norm
    vol[1] = jnp.sin(phase[...]) * norm


def finish_kernel(gathered, s, absorber, lam, zsp, spk, place, *rest, tail, first):
    damped, out, keep, am, bm = rest[-5:]
    step = pl.program_id(0)
    planes = lam.shape[0] // 2
    wz = lam.shape[1] // 2
    nx = planes

    @pl.when(step == 0)
    def _():
        left, right = chain(gathered, nx, lax.axis_index("gz"), keep)
        for x in range(planes):
            al = lam[x : x + 1, :]
            ar = lam[nx + x : nx + x + 1, :]

            def turned(row):
                return jnp.concatenate([-row[:, wz : 2 * wz], row[:, 0:wz]], 1)

            b = jnp.concatenate([al, turned(al), ar, turned(ar), zsp[0:4, :]], 0)
            a = jnp.concatenate(
                [spk[0:4, :]] + [v[x : x + 1] for v in (left[0], left[1], right[0], right[1])], 0
            )
            bhi = b.astype(bf16).astype(f32)
            ahi = a.astype(bf16).astype(f32)
            bm[x] = jnp.concatenate([bhi, b - bhi, bhi, jnp.zeros_like(b)], 0).astype(bf16)
            am[x] = jnp.concatenate([ahi, ahi, a - ahi, jnp.zeros_like(a)], 0).astype(bf16)

    sides = s.shape[0]
    groups = out.shape[0]
    rows = place.shape[1] // groups
    parts = []
    for side in range(sides):
        x = first + step * sides + side
        field = s[side] + mm(am[x], bm[x], TN)
        kept = jnp.exp(-absorber[side])
        fr = field[:, 0:wz]
        fi = field[:, wz : 2 * wz]
        dr = fr * kept
        di = fi * kept
        damped[0, side] = dr
        damped[1, side] = di
        lr = fr - dr
        li = fi - di
        folded = jnp.concatenate(
            [
                sum(lr[:, k * KZ : (k + 1) * KZ] for k in range(wz // KZ)),
                sum(li[:, k * KZ : (k + 1) * KZ] for k in range(wz // KZ)),
            ],
            1,
        )
        hi, lo = split(folded)
        parts.append(
            mm(place[side % place.shape[0]], jnp.concatenate([hi, lo], 0)).reshape(
                groups, rows, 2 * KZ
            )
        )
    if tail is None:
        for side in range(sides):
            out[:, side * rows : (side + 1) * rows, :] = parts[side]
    else:
        out[:, 0:tail, :] = parts[0][:, 0:tail]
        out[:, tail : 2 * tail, :] = parts[1][:, 0:tail]
        out[:, 2 * tail : 2 * tail + 8, :] = parts[0][:, tail:rows] + parts[1][:, tail:rows]


def transform_kernel(got, yt, ez, vol, *rest, tail):
    out = rest[-1]
    sides = out.shape[1]
    groups = got.shape[0]
    rows = yt.shape[3] // groups
    half = yt.shape[2] // 2
    for side in range(sides):
        if tail is None:
            block = got[:, side * rows : (side + 1) * rows, :]
        else:
            block = jnp.concatenate(
                [
                    got[:, side * tail : (side + 1) * tail, :],
                    got[:, 2 * tail : 2 * tail + 8, :],
                ],
                1,
            )
        u = mm3((yt[side % yt.shape[0], 0], yt[side % yt.shape[0], 1]), split(block.reshape(groups * rows, 2 * KZ)))
        ur = u[0:half, 0:KZ] - u[half:, KZ:]
        ui = u[0:half, KZ:] + u[half:, 0:KZ]
        v = mm3(split(jnp.concatenate([ur, ui], 1)), (ez[0], ez[1]))
        vr = v[:, 0:KZ]
        vi = v[:, KZ:]
        out[0, side] = vol[0] * vr - vol[1] * vi
        out[1, side] = vol[0] * vi + vol[1] * vr


def halves(table):
    exact = np.asarray(table, np.float64)
    hi = exact.astype(jnp.bfloat16)
    lo = (exact - hi.astype(np.float64)).astype(jnp.bfloat16)
    return np.stack([hi, lo])


def transform_tables():
    n = np.arange(KY)
    angle = 2.0 * np.pi / KY * (np.outer(n, n) % KY) - np.pi * (n % 2)[None, :]
    ytab = halves(np.concatenate([np.cos(angle), -np.sin(angle)], 0))
    n = np.arange(KZ)
    angle = 2.0 * np.pi / KZ * (np.outer(n, n) % KZ) - np.pi * (n % 2)[:, None]
    er, ei = np.cos(angle), -np.sin(angle)
    ztab = halves(np.block([[er, ei], [-ei, er]]))
    return ytab, ztab


def whole(shape):
    zeros = (0,) * len(shape)
    return pl.BlockSpec(tuple(shape), lambda *_: zeros)


def body(
    wavefunction,
    absorber,
    row_inverse,
    column_inverse,
    link_terms,
    shell_blocks,
    owner_map,
    volkov_phase,
):
    nx, wy, wz = wavefunction.shape[1:]
    groups = lax.axis_size("gy")
    shell = shell_blocks.shape[2]
    capacity = 2 * ((shell + groups - 1) // groups)
    sent = capacity * BY
    pair = sent % 8 == 4 and nx % 2 == 0
    sides = 2 if nx % 2 == 0 else 1
    tail = sent - 4 if pair else None
    rows = (sent + 7) // 8 * 8
    per_step = 2 * sent if pair else sides * rows
    smem = pl.BlockSpec(memory_space=pltpu.SMEM)
    listed = shell_blocks[0]
    owners = owner_map[0, :, :, 0]
    ytab, ztab = transform_tables()
    norm = 1.0 / math.sqrt(wy * wz)

    thi, tlo, pay, spk = pl.pallas_call(
        solve_rows_kernel,
        grid=(nx,),
        in_specs=[
            smem,
            pl.BlockSpec((2, 1, wy, wz), lambda x: (0, x, 0, 0)),
            whole((2, wy, wy)),
        ],
        out_specs=[
            pl.BlockSpec((1, wy, 2 * wz), lambda x: (x, 0, 0)),
            pl.BlockSpec((1, wy, 2 * wz), lambda x: (x, 0, 0)),
            whole((groups, 4 * nx + EDGE, wz)),
            whole((8, wy)),
        ],
        out_shape=[
            jax.ShapeDtypeStruct((nx, wy, 2 * wz), bf16),
            jax.ShapeDtypeStruct((nx, wy, 2 * wz), bf16),
            jax.ShapeDtypeStruct((groups, 4 * nx + EDGE, wz), f32),
            jax.ShapeDtypeStruct((8, wy), f32),
        ],
        scratch_shapes=[
            pltpu.VMEM((2 * wy, 2 * wy), bf16),
            pltpu.VMEM((2 * wy, 2 * wy), bf16),
            pltpu.VMEM((4 * nx + EDGE, wz), f32),
        ],
        name="solve_rows",
    )(link_terms, wavefunction, row_inverse)

    gathered = lax.all_to_all(pay, "gy", split_axis=0, concat_axis=0, tiled=True)

    s, base, zh, zl, zsp, zed = pl.pallas_call(
        solve_columns_kernel,
        grid=(nx,),
        in_specs=[
            smem,
            pl.BlockSpec((1, wy, 2 * wz), lambda x: (x, 0, 0)),
            pl.BlockSpec((1, wy, 2 * wz), lambda x: (x, 0, 0)),
            pl.BlockSpec(memory_space=pl.ANY),
        ],
        out_specs=[
            pl.BlockSpec((1, wy, 2 * wz), lambda x: (x, 0, 0)),
            whole((4 * nx, wy)),
            whole((2 * wz, 2 * wz)),
            whole((2 * wz, 2 * wz)),
            whole((8, 2 * wz)),
            whole((EDGE, wy)),
        ],
        out_shape=[
            jax.ShapeDtypeStruct((nx, wy, 2 * wz), f32),
            jax.ShapeDtypeStruct((4 * nx, wy), f32),
            jax.ShapeDtypeStruct((2 * wz, 2 * wz), bf16),
            jax.ShapeDtypeStruct((2 * wz, 2 * wz), bf16),
            jax.ShapeDtypeStruct((8, 2 * wz), f32),
            jax.ShapeDtypeStruct((EDGE, wy), f32),
        ],
        scratch_shapes=[
            pltpu.VMEM((2, wz, wz), f32),
            pltpu.VMEM((16, 2 * wz), bf16),
            pltpu.VMEM((16, 2 * wz), bf16),
            pltpu.SemaphoreType.DMA,
        ],
        name="solve_columns",
    )(link_terms, thi, tlo, column_inverse)

    place = pl.pallas_call(
        lambda *refs: route_kernel(*refs, tail=tail),
        out_shape=jax.ShapeDtypeStruct((2 if pair else 1, groups * rows, 2 * wy), bf16),
        name="route",
    )(listed, owners)

    lam, payz = pl.pallas_call(
        row_chain_kernel,
        out_shape=[
            jax.ShapeDtypeStruct((2 * nx, 2 * wz), f32),
            jax.ShapeDtypeStruct((4 * nx + EDGE, wy), f32),
        ],
        scratch_shapes=[pltpu.VMEM((groups, 6 * nx, wz), f32)],
        name="row_chain",
    )(gathered, zh, zl, base, zed, spk)

    edges = lax.all_gather(payz, "gz")

    yt, vol = pl.pallas_call(
        lambda *refs: table_kernel(*refs, tail=tail, norm=norm),
        out_shape=[
            jax.ShapeDtypeStruct((2 if pair else 1, 2, 2 * KY, groups * rows), bf16),
            jax.ShapeDtypeStruct((2, KY, KZ), f32),
        ],
        scratch_shapes=[pltpu.VMEM((groups * rows, KY), bf16)],
        name="tables",
    )(listed, owners, jnp.asarray(ytab), volkov_phase)

    steps = nx // sides // CHUNKS
    columns = edges.shape[0]
    sends = []
    damped = None
    for chunk in range(CHUNKS):
        start = chunk * steps

        def at(index, start=start):
            return lambda i: tuple(start + i if d == index else 0 for d in range(3))

        carried = [] if damped is None else [damped]
        damped, out = pl.pallas_call(
            lambda *refs, start=start: finish_kernel(*refs, tail=tail, first=start * sides),
            grid=(steps,),
            in_specs=[
                whole((columns, 4 * nx + EDGE, wy)),
                pl.BlockSpec((sides, wy, 2 * wz), at(0)),
                pl.BlockSpec((sides, wy, wz), at(0)),
                whole((2 * nx, 2 * wz)),
                whole((8, 2 * wz)),
                whole((8, wy)),
                whole(place.shape),
            ]
            + [pl.BlockSpec(memory_space=pl.ANY)] * len(carried),
            out_specs=[
                pl.BlockSpec((2, sides, wy, wz), lambda i, start=start: (0, start + i, 0, 0)),
                pl.BlockSpec((groups, per_step, 2 * KZ), lambda i: (0, i, 0)),
            ],
            out_shape=[
                jax.ShapeDtypeStruct((2, nx, wy, wz), f32),
                jax.ShapeDtypeStruct((groups, steps * per_step, 2 * KZ), f32),
            ],
            scratch_shapes=[
                pltpu.VMEM((columns, 6 * nx, wy), f32),
                pltpu.VMEM((nx, 32, wy), bf16),
                pltpu.VMEM((nx, 32, 2 * wz), bf16),
            ],
            input_output_aliases={7: 0} if carried else {},
            name="finish",
        )(edges, s, absorber, lam, zsp, spk, place, *carried)
        sends.append(out)

    spectrum = None
    for chunk, out in enumerate(sends):
        start = chunk * steps
        got = lax.all_to_all(out, "gy", split_axis=0, concat_axis=0, tiled=True)
        carried = [] if spectrum is None else [spectrum]
        spectrum = pl.pallas_call(
            lambda *refs: transform_kernel(*refs, tail=tail),
            grid=(steps,),
            in_specs=[
                pl.BlockSpec((groups, per_step, 2 * KZ), lambda i: (0, i, 0)),
                whole(yt.shape),
                whole(ztab.shape),
                whole((2, KY, KZ)),
            ]
            + [pl.BlockSpec(memory_space=pl.ANY)] * len(carried),
            out_specs=pl.BlockSpec(
                (2, sides, KY, KZ), lambda i, start=start: (0, start + i, 0, 0)
            ),
            out_shape=jax.ShapeDtypeStruct((2, nx, KY, KZ), f32),
            input_output_aliases={4: 0} if carried else {},
            name="transform",
        )(got, yt, jnp.asarray(ztab), vol, *carried)
    return damped, spectrum


def solution(mesh):
    placed = (
        P(None, None, "gy", "gz"),
        P(None, "gy", "gz"),
        P(None, "gy", None),
        P(),
        P(),
        P("gz", None, None),
        P("gz", None, None, None),
        P(),
    )
    return jax.shard_map(
        body,
        mesh=mesh,
        in_specs=placed,
        out_specs=(P(None, None, "gy", "gz"), P(None, "gy", "gz", None)),
        check_vma=False,
    )
```

time: 537 us -> 98.9 us (0.18); the launches traced: 529 us -> 98 us
  blocking collectives: 138 us -> 6.71 us
  local copies, waits for them, and re-layouts: 73.3 us -> 1.99 us
  loops' own time: 68 us -> 0 us
  waiting for transfers between devices: 104 us -> 40 us
  other arithmetic: 53 us -> 0 us
  matrix products: 43.6 us -> 0 us
  Pallas kernels: 0 us -> 35.4 us
  between operations: 28.7 us -> 0.66 us
  starting transfers between devices: 20.2 us -> 13.2 us
    all_gather x3 -> x1, blocking collectives: 97.3 us -> 6.71 us  [body(): edges = lax.all_gather(payz, 'gz')]
    another operation x5 -> x0, loops' own time: 68 us -> none  [the longest x1 37.7 us: chain_local(): lax.scan(forward, initial, (edges, head_part, tail_part))]
    all_to_all x5 -> x2, waiting for transfers between devices: 104 us -> 40 us  [the longest x1 40 us: body(): got = lax.all_to_all(out, 'gy', split_axis=0, concat_axis=0, tiled=True)]
    dot_general x19 -> x0, matrix products: 43.6 us -> none  [the longest x4 11.3 us: complex_einsum(): jnp.einsum(pattern, former[0], latter[1], precision=precise)]
    dynamic_slice x75 -> x0, local copies, waits for them, and re-layouts: 40 us -> none  [the longest x68 39.9 us: chain_local(): lax.scan(forward, initial, (edges, head_part, tail_part))]
    pallas_call x0 -> x7, Pallas kernels: none -> 35.4 us  [the longest x1 8.94 us: body(): pl.pallas_call(solve_columns_kernel, grid=(nx,), in_specs=[smem, pl.Block...]
    unnamed x1 -> x0, blocking collectives: 23.9 us -> none
    add x26 -> x0, other arithmetic: 23.4 us -> none  [the longest x14 11.5 us: complex_add(): return (former[0] + latter[0], former[1] + latter[1])]
  transfers between devices with their start and end apart: 5 -> 2, of which waited for: 5 -> 1; matrix products, arithmetic and copies ran while one was open for 5% -> 0% of each run, Pallas kernels for 0% -> 14%
where the time goes in v1:
time: 98.9 us; the launch traced here: 98 us
  waiting for transfers between devices  40 us (40%)
  Pallas kernels  35.4 us (36%)
  starting transfers between devices  13.2 us (13%)
  blocking collectives  6.71 us (7%)
  local copies, waits for them, and re-layouts  1.99 us (2%)
    all_to_all x1, waiting for transfers between devices, body(): got = lax.all_to_all(out, 'gy', split_axis=0, concat_axis=0, tiled=True)  40 us
    pallas_call x1, Pallas kernels, body(): pl.pallas_call(solve_columns_kernel, grid=(nx,), in_specs=[smem, pl.Block...  8.94 us
    all_to_all x1, starting transfers between devices, body(): lax.all_to_all(pay, 'gy', split_axis=0, concat_axis=0, tiled=True)  7.32 us
    pallas_call x1, Pallas kernels, body(): pl.pallas_call(solve_rows_kernel, grid=(nx,), in_specs=[smem, pl.BlockSpe...  7 us
    all_gather x1, blocking collectives, body(): edges = lax.all_gather(payz, 'gz')  6.71 us
    pallas_call x1, Pallas kernels, body(): pl.pallas_call(lambda *refs: transform_kernel(*refs, tail=tail), grid=(st...  5.99 us
    pallas_call x1, Pallas kernels, body(): pl.pallas_call(lambda *refs, start=start: finish_kernel(*refs, tail=tail,...  5.98 us
    all_to_all x1, starting transfers between devices, body(): got = lax.all_to_all(out, 'gy', split_axis=0, concat_axis=0, tiled=True)  5.88 us
  transfers between devices with their start and end apart: 2, of which 1 were waited for; matrix products, arithmetic and copies ran while one was open for 0% of the time, Pallas kernels for 14%

profile of v1, /device:TPU:0, one launch (start us, length us, event | category | flops | bytes accessed | tf_op | source)
XLA Modules:
  0.0 98.0 jit_solution(9974273486130088242)
XLA Ops:
  0.6 7.0 %solve_rows.1 = (bf16[8,128,512]{2,1,0:T(8,128)(2,1)}, bf16[8,128,512]{2,1,0:T(8,128)(2,1)}, f32[8,40,256]{2,1,0:T(8,128)}, f32[8,128]{1,0:T(8,128)}) custom-call(f32[2,2,2]{2,1,0:T(2,128)} %link.3, f32[2,8,128,256]{3,2,1,0:T(8,128)} %w.1, f32[2,128,128]{2,1,0:T(8,128)} %y.1), custom_call_target="tpu_custom_call" | custom-call | tf_op jit(solution)/shard_map/solve_rows/pallas_call | solution.py:435
  7.6 7.3 %all-to-all-start = ((f32[8,40,256]{2,1,0:T(8,128)}), f32[8,40,256]{2,1,0:T(8,128)S(1)}, u32[]{:S(2)}, u32[]{:S(2)}) async-start(f32[8,40,256]{2,1,0:T(8,128)} %get-tuple-element.18), calls=%async_computation | async-start | bytes 655360 | tf_op jit(solution)/shard_map/all_to_all | solution.py:463
  15.0 1.8 %route.1.refs_6_ = bf16[2,256,256]{2,1,0:T(8,128)(2,1)} custom-call(s32[8,56]{1,0:T(8,128)} %bitcast.4, s32[8,56]{1,0:T(8,128)} %bitcast.6), custom_call_target="tpu_custom_call" | custom-call | tf_op jit(solution)/shard_map/route/pallas_call | solution.py:499
  16.7 8.9 %solve_columns.1 = (f32[8,128,512]{2,1,0:T(8,128)}, f32[32,128]{1,0:T(8,128)}, bf16[512,512]{1,0:T(8,128)(2,1)}, bf16[512,512]{1,0:T(8,128)(2,1)}, f32[8,512]{1,0:T(8,128)}, /*index=5*/f32[8,128]{1,0:T(8,128)}) custom-call(f32[2,2,2]{2,1,0:T(2,128)} %link.3, bf16[8,128,512]{2,1,0:T(8,128)(2,1)} %get-tuple-element.19.thi, ...), custom_call_target="tpu_custom_call" | custom-call | tf_op jit(solution)/shard_map/solve_columns/pallas_call | solution.py:465
  25.7 0.0 all-to-all-done.gathered
  25.7 0.0 copy-start.1
  25.7 0.7 copy-done.1
  26.4 2.6 %row_chain.1 = (f32[16,512]{1,0:T(8,128)}, f32[40,128]{1,0:T(8,128)}) custom-call(f32[8,40,256]{2,1,0:T(8,128)} %copy-done.1, bf16[512,512]{1,0:T(8,128)(2,1)} %get-tuple-element.21.zh, bf16[512,512]{1,0:T(8,128)(2,1)} %get-tuple-element.22.zl, f32[32,128]{1,0:T(8,128)} %get-tuple-element.23.base, f32[8,128]{1,0:T(8,128)} %get-tuple-element.24.zed, ...), custom_call_target="tpu_custom_call" | custom-call | tf_op jit(solution)/shard_map/row_chain/pallas_call | solution.py:505
  29.0 6.7 %all-gather = f32[160,128]{1,0:T(8,128)} all-gather(f32[40,128]{1,0:T(8,128)} %get-tuple-element.26), channel_id=2, replica_groups=mesh['gy'=8,'gz'=4] {'gz'}, dimensions={0}, use_global_device_ids=true | all-gather | bytes 102400 | tf_op jit(solution)/shard_map/all_gather | solution.py:515
  35.7 6.0 %finish.1 = (f32[2,8,128,256]{3,2,1,0:T(8,128)}, f32[8,224,256]{2,1,0:T(8,128)}) custom-call(f32[4,40,128]{2,1,0:T(8,128)} %bitcast.3, f32[8,128,512]{2,1,0:T(8,128)} %get-tuple-element.27.refs_1_, f32[8,128,256]{2,1,0:T(8,128)} %refs_2_.3, f32[16,512]{1,0:T(8,128)} %get-tuple-element.28.refs_3_, f32[8,512]{1,0:T(8,128)} %get-tuple-element.29.refs_4_, ...), custom_call_target="tpu_custom_call" | custom-call | tf_op jit(solution)/shard_map/finish/pallas_call | solution.py:538
  41.7 5.9 %all-to-all-start.1 = ((f32[8,224,256]{2,1,0:T(8,128)}), f32[8,224,256]{2,1,0:T(8,128)S(1)}, u32[]{:S(2)}, u32[]{:S(2)}) async-start(f32[8,224,256]{2,1,0:T(8,128)} %get-tuple-element.31), calls=%async_computation.1 | async-start | bytes 3670016 | tf_op jit(solution)/shard_map/all_to_all | solution.py:572
  47.6 3.1 %tables.1 = (bf16[2,2,256,256]{3,2,1,0:T(8,128)(2,1)}, f32[2,128,128]{2,1,0:T(8,128)}) custom-call(s32[8,56]{1,0:T(8,128)} %bitcast.5, s32[8,56]{1,0:T(8,128)} %bitcast.7, bf16[2,256,128]{2,1,0:T(8,128)(2,1)} %constant.4.clone.refs_2_, f32[128,128]{1,0:T(8,128)} %refs_3_.1), custom_call_target="tpu_custom_call" | custom-call | tf_op jit(solution)/shard_map/tables/pallas_call | solution.py:517
  50.7 40.0 %all-to-all-done.1.refs_0_ = f32[8,224,256]{2,1,0:T(8,128)S(1)} async-done(((f32[8,224,256]{2,1,0:T(8,128)}), f32[8,224,256]{2,1,0:T(8,128)S(1)}, u32[]{:S(2)}, u32[]{:S(2)}) %all-to-all-start.1) | async-done | bytes 1835040 | tf_op jit(solution)/shard_map/all_to_all | solution.py:572
  90.7 0.0 copy-start
  90.7 1.3 %copy-done = f32[8,224,256]{2,1,0:T(8,128)} copy-done((f32[8,224,256]{2,1,0:T(8,128)}, f32[8,224,256]{2,1,0:T(8,128)S(1)}, u32[]{:S(2)}) %copy-start) | copy-done | bytes 1835032
  92.0 6.0 %transform.1 = f32[2,8,128,128]{3,2,1,0:T(8,128)} custom-call(f32[8,224,256]{2,1,0:T(8,128)} %copy-done, bf16[2,2,256,256]{3,2,1,0:T(8,128)(2,1)} %get-tuple-element.32.refs_1_, bf16[2,256,256]{2,1,0:T(8,128)(2,1)} %constant.5.clone.refs_2_, f32[2,128,128]{2,1,0:T(8,128)} %get-tuple-element.33.refs_3_), custom_call_target="tpu_custom_call" | custom-call | tf_op jit(solution)/shard_map/transform/pallas_call | solution.py:574
Async XLA Ops:
  7.6 18.0 %all-to-all-start = ((f32[8,40,256]{2,1,0:T(8,128)}), f32[8,40,256]{2,1,0:T(8,128)S(1)}, u32[]{:S(2)}, u32[]{:S(2)}) async-start(f32[8,40,256]{2,1,0:T(8,128)} %get-tuple-element.18), calls=%async_computation | async-start | bytes 655360 | tf_op jit(solution)/shard_map/all_to_all | solution.py:463
  25.7 0.7 copy-start.1
  41.7 49.0 %all-to-all-start.1 = ((f32[8,224,256]{2,1,0:T(8,128)}), f32[8,224,256]{2,1,0:T(8,128)S(1)}, u32[]{:S(2)}, u32[]{:S(2)}) async-start(f32[8,224,256]{2,1,0:T(8,128)} %get-tuple-element.31), calls=%async_computation.1 | async-start | bytes 3670016 | tf_op jit(solution)/shard_map/all_to_all | solution.py:572
  90.7 1.3 %copy-start = (f32[8,224,256]{2,1,0:T(8,128)}, f32[8,224,256]{2,1,0:T(8,128)S(1)}, u32[]{:S(2)}) copy-start(f32[8,224,256]{2,1,0:T(8,128)S(1)} %all-to-all-done.1.refs_0_) | copy-start | bytes 5505028
